TPU v7x, 32 devices: a whole 2x2x4 slice. The times are simulated.
32 devices in a mesh: gx: 4 (over z), gy: 4 (over x, core), gz: 2 (over y).
Axes of the slice: x: 2, y: 2, z: 4, core: 2. Of those that a mesh axis runs over, the one named last changes fastest.
Arguments:
- krylov_basis: float32 [60, 16, 32, 256], P(None, 'gx', 'gy', 'gz'), may hold values from -6 to 6
- schur_vectors: float32 [60, 20], replicated, may hold values from -1 to 1, as said below
- next_vector: float32 [16, 32, 256], P('gx', 'gy', 'gz'), may hold values from -10 to 10
- diag_shift: float32 [16, 32, 256], P('gx', 'gy', 'gz'), may hold values from 0.25 to 2
- velocity: float32 [3, 16, 32, 256], P(None, 'gx', 'gy', 'gz'), may hold values from -1 to 1
Outputs:
- new_basis: float32 [24, 16, 32, 256], P(None, 'gx', 'gy', 'gz')
- hessenberg: float32 [24, 3], replicated
Inputs may be any that keep to these rules, and one draw needn't show every extreme that they name: `schur_vectors`: the columns are orthonormal.
All inputs are finite; a program needn't handle non-finite values.
Results may differ from a plain program's by a relative error of at most 0.0003.
Values sent between devices are 32-bit elements; how exact they have to be, the bound alone decides.
A program may use at most 64 MiB of HBM per device.

v0:
```python
import jax
import jax.numpy as jnp
from jax import lax
from jax.sharding import PartitionSpec as P

KEEP = 20
EXPAND = 3
ROWS = 24


def with_halo(value, sides, width):
    for axis, dim in sides:
        count, length = (lax.axis_size(axis), value.shape[dim])
        up = [(i, (i + 1) % count) for i in range(count - 1)]
        down = [(j, i) for i, j in up]
        last = lax.slice_in_dim(value, length - width, length, axis=dim)
        initial = lax.slice_in_dim(value, 0, width, axis=dim)
        before = lax.ppermute(last, axis, up)
        after = lax.ppermute(initial, axis, down)
        value = jnp.concatenate([before, value, after], axis=dim)
    return value


def combine_terms(
    field, x_ahead, x_behind, y_ahead, y_behind, z_ahead, z_behind, diag_shift, velocity
):
    neighbours = x_ahead + x_behind + y_ahead + y_behind + z_ahead + z_behind
    flow = (
        velocity[0] * (x_ahead - x_behind)
        + velocity[1] * (y_ahead - y_behind)
        + velocity[2] * (z_ahead - z_behind)
    )
    return (6.0 + diag_shift) * field - neighbours + 0.5 * flow


def operate_field(field, diag_shift, velocity):
    padded = with_halo(field, (("gx", 0), ("gy", 1), ("gz", 2)), 1)
    return combine_terms(
        field,
        padded[2:, 1:-1, 1:-1],
        padded[:-2, 1:-1, 1:-1],
        padded[1:-1, 2:, 1:-1],
        padded[1:-1, :-2, 1:-1],
        padded[1:-1, 1:-1, 2:],
        padded[1:-1, 1:-1, :-2],
        diag_shift,
        velocity,
    )


def per_device(krylov_basis, schur_vectors, next_vector, diag_shift, velocity):
    highest = lax.Precision.HIGHEST
    shape_local = next_vector.shape
    cell_count = (
        shape_local[0]
        * shape_local[1]
        * shape_local[2]
        * lax.axis_size("gx")
        * lax.axis_size("gy")
        * lax.axis_size("gz")
    )
    rotated = jnp.einsum("ik,ixyz->kxyz", schur_vectors, krylov_basis, precision=highest)
    columns = []
    starting = jnp.concatenate([rotated, next_vector[None]], axis=0)
    flat_start = starting.reshape(KEEP + 1, -1)
    gram_matrix = (
        lax.psum(jnp.dot(flat_start, flat_start.T, precision=highest), ("gx", "gy", "gz"))
        / cell_count
    )
    divisor = jnp.maximum(jnp.sqrt(gram_matrix[KEEP, KEEP]), 0.5)
    factor = jnp.ones((KEEP + 1,), jnp.float32).at[KEEP].set(1.0 / divisor)
    gram_matrix = gram_matrix * factor[:, None] * factor[None, :]
    vectors = jnp.concatenate([rotated, (next_vector / divisor)[None]], axis=0)
    for expansion in range(EXPAND):
        count = vectors.shape[0]
        flat_basis = vectors.reshape(count, -1)
        applied = operate_field(vectors[-1], diag_shift, velocity).reshape(-1)
        dotted, self_sum = lax.psum(
            (jnp.dot(flat_basis, applied, precision=highest), jnp.sum(applied * applied)),
            ("gx", "gy", "gz"),
        )
        first_coeffs = dotted / cell_count
        self_norm = self_sum / cell_count
        second_coeffs = first_coeffs - jnp.dot(gram_matrix, first_coeffs, precision=highest)
        total_coeffs = first_coeffs + second_coeffs
        partly = applied - jnp.dot(first_coeffs, flat_basis, precision=highest)
        cleaned = partly - jnp.dot(second_coeffs, flat_basis, precision=highest)
        length_sq = (
            self_norm
            - 2.0 * jnp.dot(total_coeffs, first_coeffs, precision=highest)
            + jnp.dot(
                total_coeffs,
                jnp.dot(gram_matrix, total_coeffs, precision=highest),
                precision=highest,
            )
        )
        length = jnp.sqrt(jnp.maximum(length_sq, 0.0))
        divisor = jnp.maximum(length, 0.5)
        column = jnp.zeros((ROWS,), jnp.float32)
        column = column.at[:count].set(total_coeffs).at[count].set(length)
        columns.append(column)
        newest = (cleaned / divisor).reshape(shape_local)
        vectors = jnp.concatenate([vectors, newest[None]], axis=0)
        intersect = (
            second_coeffs - jnp.dot(gram_matrix, second_coeffs, precision=highest)
        ) / divisor
        corner = jnp.maximum(length_sq, 0.0) / (divisor * divisor)
        upper_rows = jnp.concatenate([gram_matrix, intersect[:, None]], axis=1)
        lower_row = jnp.concatenate([intersect, corner[None]], axis=0)
        gram_matrix = jnp.concatenate([upper_rows, lower_row[None]], axis=0)
    return (vectors, jnp.stack(columns, axis=1))


def solution(mesh):
    in_specs = (
        P(None, "gx", "gy", "gz"),
        P(),
        P("gx", "gy", "gz"),
        P("gx", "gy", "gz"),
        P(None, "gx", "gy", "gz"),
    )
    out_specs = (P(None, "gx", "gy", "gz"), P())
    return jax.shard_map(
        per_device, mesh=mesh, in_specs=in_specs, out_specs=out_specs, check_vma=False
    )
```

profile of v0, /device:TPU:0, one launch (start us, length us, event | category | flops | bytes accessed | tf_op | source)
XLA Modules:
  0.0 258.3 jit_solution(9260418553971904028)
XLA Ops:
  0.7 1.2 copy-done
  1.8 1.9 fusion.10
  3.7 0.5 convolution_bitcast_fusion
  4.2 42.1 %psum.49 = f32[21,21]{1,0:T(8,128)S(1)} all-reduce(f32[21,21]{1,0:T(8,128)S(1)} %convolution_bitcast_fusion), channel_id=1, replica_groups=mesh['gx'=4,'gy'=4,'gz'=2] {'gx','gy','gz'}, use_global_device_ids=true, to_apply=%region_0.0 | all-reduce | flops 441 | bytes 3528 | tf_op jit(solution)/shard_map/psum | solution.py:67
  46.3 0.6 slice.304
  47.6 1.3 collective-permute-start
  48.9 4.5 %collective-permute-start.1 = (f32[1,8,128]{2,1,0:T(8,128)S(1)}, f32[1,8,128]{2,1,0:T(8,128)S(1)}, u32[]{:S(2)}, u32[]{:S(2)}) collective-permute-start(f32[1,8,128]{2,1,0:T(8,128)S(1)} %get-tuple-element.124), channel_id=1, source_target_pairs={{0,8},{8,16},{16,24},{1,9},{9,17},{17,25},{2,10},{10,18},{18,26},{... | collective-permute-start | bytes 12296 | tf_op jit(solution)/shard_map/ppermute | solution.py:18
  53.7 1.1 collective-permute-done.1
  54.8 1.3 collective-permute-start.2
  56.1 3.0 %collective-permute-start.3 = (f32[6,1,128]{2,1,0:T(1,128)S(1)}, f32[6,1,128]{2,1,0:T(1,128)S(1)}, u32[]{:S(2)}, u32[]{:S(2)}) collective-permute-start(f32[6,1,128]{2,1,0:T(1,128)S(1)} %get-tuple-element.118), channel_id=1, source_target_pairs={{0,2},{2,4},{4,6},{1,3},{3,5},{5,7},{8,10},{10,12},{12,14},{9,11},... | collective-permute-start | bytes 9224 | tf_op jit(solution)/shard_map/ppermute | solution.py:18
  59.3 0.7 collective-permute-done.3
  60.0 4.2 %collective-permute-start.5 = (f32[6,10,1]{2,1,0:T(8,128)S(1)}, f32[6,10,1]{2,1,0:T(8,128)S(1)}, u32[]{:S(2)}, u32[]{:S(2)}) collective-permute-start(f32[6,10,1]{2,1,0:T(8,128)S(1)} %get-tuple-element.113), channel_id=1, source_target_pairs={{0,1},{2,3},{4,5},{6,7},{8,9},{10,11},{12,13},{14,15},{16,17},{18,... | collective-permute-start | bytes 728 | tf_op jit(solution)/shard_map/ppermute | solution.py:18
  64.2 1.3 collective-permute-start.4
  65.6 0.2 copy.36
  65.8 0.1 collective-permute-done.5
  66.0 4.3 %collective-permute-done.4 = f32[6,10,1]{2,1,0:T(8,128)S(1)} collective-permute-done((f32[6,10,1]{2,1,0:T(8,128)S(1)}, f32[6,10,1]{2,1,0:T(8,128)S(1)}, u32[]{:S(2)}, u32[]{:S(2)}) %collective-permute-start.4) | collective-permute-done | bytes 272 | tf_op jit(solution)/shard_map/ppermute | solution.py:19
  70.2 0.7 multiply_reduce_fusion.2
  70.9 0.5 convolution_bitcast_fusion.11
  71.4 40.6 %all-reduce.6 = (f32[21]{0:T(128)S(1)}, f32[]{:T(128)}) all-reduce(f32[21]{0:T(128)S(1)} %convolution_bitcast_fusion.11, f32[]{:T(128)} %get-tuple-element.106), channel_id=1, replica_groups=mesh['gx'=4,'gy'=4,'gz'=2] {'gx','gy','gz'}, use_global_device_ids=true, to_apply=%region_1.0 | all-reduce | flops 22 | bytes 176 | tf_op jit(solution)/shard_map/psum | solution.py:78
  112.0 0.7 multiply_reduce_fusion.5
  112.7 0.3 fusion.34
  113.1 0.3 fusion.33
  114.1 0.7 fusion.12
  116.2 0.1 fusion.8
  116.3 1.3 collective-permute-start.6
  117.6 4.5 %collective-permute-start.7 = (f32[1,8,128]{2,1,0:T(8,128)S(1)}, f32[1,8,128]{2,1,0:T(8,128)S(1)}, u32[]{:S(2)}, u32[]{:S(2)}) collective-permute-start(f32[1,8,128]{2,1,0:T(8,128)S(1)} %get-tuple-element.122), channel_id=1, source_target_pairs={{0,8},{8,16},{16,24},{1,9},{9,17},{17,25},{2,10},{10,18},{18,26},{... | collective-permute-start | bytes 12296 | tf_op jit(solution)/shard_map/ppermute | solution.py:18
  122.5 1.0 collective-permute-done.7
  123.5 1.3 collective-permute-start.8
  124.8 3.0 %collective-permute-start.9 = (f32[6,1,128]{2,1,0:T(1,128)S(1)}, f32[6,1,128]{2,1,0:T(1,128)S(1)}, u32[]{:S(2)}, u32[]{:S(2)}) collective-permute-start(f32[6,1,128]{2,1,0:T(1,128)S(1)} %get-tuple-element.116), channel_id=1, source_target_pairs={{0,2},{2,4},{4,6},{1,3},{3,5},{5,7},{8,10},{10,12},{12,14},{9,11},... | collective-permute-start | bytes 9224 | tf_op jit(solution)/shard_map/ppermute | solution.py:18
  127.8 0.8 collective-permute-done.9
  128.7 4.4 %collective-permute-start.11 = (f32[6,10,1]{2,1,0:T(8,128)S(1)}, f32[6,10,1]{2,1,0:T(8,128)S(1)}, u32[]{:S(2)}, u32[]{:S(2)}) collective-permute-start(f32[6,10,1]{2,1,0:T(8,128)S(1)} %get-tuple-element.111), channel_id=1, source_target_pairs={{0,1},{2,3},{4,5},{6,7},{8,9},{10,11},{12,13},{14,15},{16,17},{18,... | collective-permute-start | bytes 728 | tf_op jit(solution)/shard_map/ppermute | solution.py:18
  133.1 1.3 collective-permute-start.10
  134.4 0.1 scatter.26
  134.5 0.3 collective-permute-done.11
  134.8 4.5 %collective-permute-done.10 = f32[6,10,1]{2,1,0:T(8,128)S(1)} collective-permute-done((f32[6,10,1]{2,1,0:T(8,128)S(1)}, f32[6,10,1]{2,1,0:T(8,128)S(1)}, u32[]{:S(2)}, u32[]{:S(2)}) %collective-permute-start.10) | collective-permute-done | bytes 272 | tf_op jit(solution)/shard_map/ppermute | solution.py:19
  139.4 0.7 multiply_reduce_fusion.1
  140.1 0.5 convolution_bitcast_fusion.10
  140.5 41.6 %all-reduce.5 = (f32[22]{0:T(128)S(1)}, f32[]{:T(128)}) all-reduce(f32[22]{0:T(128)S(1)} %convolution_bitcast_fusion.10, f32[]{:T(128)} %get-tuple-element.102), channel_id=1, replica_groups=mesh['gx'=4,'gy'=4,'gz'=2] {'gx','gy','gz'}, use_global_device_ids=true, to_apply=%region_4.0 | all-reduce | flops 23 | bytes 184 | tf_op jit(solution)/shard_map/psum | solution.py:78
  182.1 0.7 multiply_reduce_fusion.4
  182.9 0.4 fusion.36
  183.2 0.4 fusion.35
  184.9 0.7 fusion.13
  186.3 0.1 fusion.9
  186.5 1.3 collective-permute-start.12
  187.8 4.5 %collective-permute-start.13 = (f32[1,8,128]{2,1,0:T(8,128)S(1)}, f32[1,8,128]{2,1,0:T(8,128)S(1)}, u32[]{:S(2)}, u32[]{:S(2)}) collective-permute-start(f32[1,8,128]{2,1,0:T(8,128)S(1)} %get-tuple-element.120), channel_id=1, source_target_pairs={{0,8},{8,16},{16,24},{1,9},{9,17},{17,25},{2,10},{10,18},{18,26},{... | collective-permute-start | bytes 12296 | tf_op jit(solution)/shard_map/ppermute | solution.py:18
  192.6 1.0 collective-permute-done.13
  193.7 1.3 collective-permute-start.14
  195.0 3.0 %collective-permute-start.15 = (f32[6,1,128]{2,1,0:T(1,128)S(1)}, f32[6,1,128]{2,1,0:T(1,128)S(1)}, u32[]{:S(2)}, u32[]{:S(2)}) collective-permute-start(f32[6,1,128]{2,1,0:T(1,128)S(1)} %get-tuple-element.114), channel_id=1, source_target_pairs={{0,2},{2,4},{4,6},{1,3},{3,5},{5,7},{8,10},{10,12},{12,14},{9,11},... | collective-permute-start | bytes 9224 | tf_op jit(solution)/shard_map/ppermute | solution.py:18
  198.0 0.8 collective-permute-done.15
  198.9 4.4 %collective-permute-start.17 = (f32[6,10,1]{2,1,0:T(8,128)S(1)}, f32[6,10,1]{2,1,0:T(8,128)S(1)}, u32[]{:S(2)}, u32[]{:S(2)}) collective-permute-start(f32[6,10,1]{2,1,0:T(8,128)S(1)} %get-tuple-element.109), channel_id=1, source_target_pairs={{0,1},{2,3},{4,5},{6,7},{8,9},{10,11},{12,13},{14,15},{16,17},{18,... | collective-permute-start | bytes 728 | tf_op jit(solution)/shard_map/ppermute | solution.py:18
  203.3 1.3 collective-permute-start.16
  204.6 0.1 scatter.30
  204.7 0.3 collective-permute-done.17
  205.0 4.5 %collective-permute-done.16 = f32[6,10,1]{2,1,0:T(8,128)S(1)} collective-permute-done((f32[6,10,1]{2,1,0:T(8,128)S(1)}, f32[6,10,1]{2,1,0:T(8,128)S(1)}, u32[]{:S(2)}, u32[]{:S(2)}) %collective-permute-start.16) | collective-permute-done | bytes 272 | tf_op jit(solution)/shard_map/ppermute | solution.py:19
  209.5 0.7 multiply_reduce_fusion
  210.2 0.5 convolution_bitcast_fusion.9
  210.7 41.6 %all-reduce.4 = (f32[23]{0:T(128)S(1)}, f32[]{:T(128)}) all-reduce(f32[23]{0:T(128)S(1)} %convolution_bitcast_fusion.9, f32[]{:T(128)} %get-tuple-element.98), channel_id=1, replica_groups=mesh['gx'=4,'gy'=4,'gz'=2] {'gx','gy','gz'}, use_global_device_ids=true, to_apply=%region_7.0 | all-reduce | flops 24 | bytes 192 | tf_op jit(solution)/shard_map/psum | solution.py:78
  252.3 0.7 multiply_reduce_fusion.3
  253.0 0.8 fusion.14
  253.8 0.4 fusion.38
  254.2 0.4 fusion.37
  256.5 0.2 concatenate.183
  256.8 0.8 copy.15
  257.7 0.6 pad_maximum_fusion.77
  (44 shorter events, 1.3 us)
Async XLA Ops:
  0.6 1.2 copy-start
  0.6 3.1 %copy-start.3 = (f32[4,8,128]{2,1,0:T(8,128)S(1)}, f32[4,8,128]{2,1,0:T(8,128)}, u32[]{:S(2)}) copy-start(f32[4,8,128]{2,1,0:T(8,128)} %param.21) | copy-start | bytes 49156
  47.6 6.1 %collective-permute-start = (f32[1,8,128]{2,1,0:T(8,128)S(1)}, f32[1,8,128]{2,1,0:T(8,128)S(1)}, u32[]{:S(2)}, u32[]{:S(2)}) collective-permute-start(f32[1,8,128]{2,1,0:T(8,128)S(1)} %get-tuple-element.125), channel_id=1, source_target_pairs={{8,0},{16,8},{24,16},{9,1},{17,9},{25,17},{10,2},{18,10},{26,18},{... | collective-permute-start | bytes 12296 | tf_op jit(solution)/shard_map/ppermute | solution.py:19
  48.9 5.9 %collective-permute-start.1 = (f32[1,8,128]{2,1,0:T(8,128)S(1)}, f32[1,8,128]{2,1,0:T(8,128)S(1)}, u32[]{:S(2)}, u32[]{:S(2)}) collective-permute-start(f32[1,8,128]{2,1,0:T(8,128)S(1)} %get-tuple-element.124), channel_id=1, source_target_pairs={{0,8},{8,16},{16,24},{1,9},{9,17},{17,25},{2,10},{10,18},{18,26},{... | collective-permute-start | bytes 12296 | tf_op jit(solution)/shard_map/ppermute | solution.py:18
  54.8 4.5 %collective-permute-start.2 = (f32[6,1,128]{2,1,0:T(1,128)S(1)}, f32[6,1,128]{2,1,0:T(1,128)S(1)}, u32[]{:S(2)}, u32[]{:S(2)}) collective-permute-start(f32[6,1,128]{2,1,0:T(1,128)S(1)} %get-tuple-element.119), channel_id=1, source_target_pairs={{2,0},{4,2},{6,4},{3,1},{5,3},{7,5},{10,8},{12,10},{14,12},{11,9},... | collective-permute-start | bytes 9224 | tf_op jit(solution)/shard_map/ppermute | solution.py:19
  56.1 3.8 %collective-permute-start.3 = (f32[6,1,128]{2,1,0:T(1,128)S(1)}, f32[6,1,128]{2,1,0:T(1,128)S(1)}, u32[]{:S(2)}, u32[]{:S(2)}) collective-permute-start(f32[6,1,128]{2,1,0:T(1,128)S(1)} %get-tuple-element.118), channel_id=1, source_target_pairs={{0,2},{2,4},{4,6},{1,3},{3,5},{5,7},{8,10},{10,12},{12,14},{9,11},... | collective-permute-start | bytes 9224 | tf_op jit(solution)/shard_map/ppermute | solution.py:18
  60.0 5.9 %collective-permute-start.5 = (f32[6,10,1]{2,1,0:T(8,128)S(1)}, f32[6,10,1]{2,1,0:T(8,128)S(1)}, u32[]{:S(2)}, u32[]{:S(2)}) collective-permute-start(f32[6,10,1]{2,1,0:T(8,128)S(1)} %get-tuple-element.113), channel_id=1, source_target_pairs={{0,1},{2,3},{4,5},{6,7},{8,9},{10,11},{12,13},{14,15},{16,17},{18,... | collective-permute-start | bytes 728 | tf_op jit(solution)/shard_map/ppermute | solution.py:18
  64.2 6.0 %collective-permute-start.4 = (f32[6,10,1]{2,1,0:T(8,128)S(1)}, f32[6,10,1]{2,1,0:T(8,128)S(1)}, u32[]{:S(2)}, u32[]{:S(2)}) collective-permute-start(f32[6,10,1]{2,1,0:T(8,128)S(1)} %get-tuple-element.112), channel_id=1, source_target_pairs={{1,0},{3,2},{5,4},{7,6},{9,8},{11,10},{13,12},{15,14},{17,16},{19,... | collective-permute-start | bytes 728 | tf_op jit(solution)/shard_map/ppermute | solution.py:19
  65.6 4.6 %copy-start.1 = (f32[3,4,8,128]{3,2,1,0:T(8,128)S(1)}, f32[3,4,8,128]{3,2,1,0:T(8,128)}, u32[]{:S(2)}) copy-start(f32[3,4,8,128]{3,2,1,0:T(8,128)} %param.23) | copy-start | bytes 147460
  65.6 4.6 %copy-start.2 = (f32[4,8,128]{2,1,0:T(8,128)S(1)}, f32[4,8,128]{2,1,0:T(8,128)}, u32[]{:S(2)}) copy-start(f32[4,8,128]{2,1,0:T(8,128)} %param.22) | copy-start | bytes 49156
  116.3 6.2 %collective-permute-start.6 = (f32[1,8,128]{2,1,0:T(8,128)S(1)}, f32[1,8,128]{2,1,0:T(8,128)S(1)}, u32[]{:S(2)}, u32[]{:S(2)}) collective-permute-start(f32[1,8,128]{2,1,0:T(8,128)S(1)} %get-tuple-element.123), channel_id=1, source_target_pairs={{8,0},{16,8},{24,16},{9,1},{17,9},{25,17},{10,2},{18,10},{26,18},{... | collective-permute-start | bytes 12296 | tf_op jit(solution)/shard_map/ppermute | solution.py:19
  117.6 5.9 %collective-permute-start.7 = (f32[1,8,128]{2,1,0:T(8,128)S(1)}, f32[1,8,128]{2,1,0:T(8,128)S(1)}, u32[]{:S(2)}, u32[]{:S(2)}) collective-permute-start(f32[1,8,128]{2,1,0:T(8,128)S(1)} %get-tuple-element.122), channel_id=1, source_target_pairs={{0,8},{8,16},{16,24},{1,9},{9,17},{17,25},{2,10},{10,18},{18,26},{... | collective-permute-start | bytes 12296 | tf_op jit(solution)/shard_map/ppermute | solution.py:18
  123.5 4.3 %collective-permute-start.8 = (f32[6,1,128]{2,1,0:T(1,128)S(1)}, f32[6,1,128]{2,1,0:T(1,128)S(1)}, u32[]{:S(2)}, u32[]{:S(2)}) collective-permute-start(f32[6,1,128]{2,1,0:T(1,128)S(1)} %get-tuple-element.117), channel_id=1, source_target_pairs={{2,0},{4,2},{6,4},{3,1},{5,3},{7,5},{10,8},{12,10},{14,12},{11,9},... | collective-permute-start | bytes 9224 | tf_op jit(solution)/shard_map/ppermute | solution.py:19
  124.8 3.8 %collective-permute-start.9 = (f32[6,1,128]{2,1,0:T(1,128)S(1)}, f32[6,1,128]{2,1,0:T(1,128)S(1)}, u32[]{:S(2)}, u32[]{:S(2)}) collective-permute-start(f32[6,1,128]{2,1,0:T(1,128)S(1)} %get-tuple-element.116), channel_id=1, source_target_pairs={{0,2},{2,4},{4,6},{1,3},{3,5},{5,7},{8,10},{10,12},{12,14},{9,11},... | collective-permute-start | bytes 9224 | tf_op jit(solution)/shard_map/ppermute | solution.py:18
  128.7 6.1 %collective-permute-start.11 = (f32[6,10,1]{2,1,0:T(8,128)S(1)}, f32[6,10,1]{2,1,0:T(8,128)S(1)}, u32[]{:S(2)}, u32[]{:S(2)}) collective-permute-start(f32[6,10,1]{2,1,0:T(8,128)S(1)} %get-tuple-element.111), channel_id=1, source_target_pairs={{0,1},{2,3},{4,5},{6,7},{8,9},{10,11},{12,13},{14,15},{16,17},{18,... | collective-permute-start | bytes 728 | tf_op jit(solution)/shard_map/ppermute | solution.py:18
  133.1 6.3 %collective-permute-start.10 = (f32[6,10,1]{2,1,0:T(8,128)S(1)}, f32[6,10,1]{2,1,0:T(8,128)S(1)}, u32[]{:S(2)}, u32[]{:S(2)}) collective-permute-start(f32[6,10,1]{2,1,0:T(8,128)S(1)} %get-tuple-element.110), channel_id=1, source_target_pairs={{1,0},{3,2},{5,4},{7,6},{9,8},{11,10},{13,12},{15,14},{17,16},{19,... | collective-permute-start | bytes 728 | tf_op jit(solution)/shard_map/ppermute | solution.py:19
  186.5 6.2 %collective-permute-start.12 = (f32[1,8,128]{2,1,0:T(8,128)S(1)}, f32[1,8,128]{2,1,0:T(8,128)S(1)}, u32[]{:S(2)}, u32[]{:S(2)}) collective-permute-start(f32[1,8,128]{2,1,0:T(8,128)S(1)} %get-tuple-element.121), channel_id=1, source_target_pairs={{8,0},{16,8},{24,16},{9,1},{17,9},{25,17},{10,2},{18,10},{26,18},{... | collective-permute-start | bytes 12296 | tf_op jit(solution)/shard_map/ppermute | solution.py:19
  187.8 5.9 %collective-permute-start.13 = (f32[1,8,128]{2,1,0:T(8,128)S(1)}, f32[1,8,128]{2,1,0:T(8,128)S(1)}, u32[]{:S(2)}, u32[]{:S(2)}) collective-permute-start(f32[1,8,128]{2,1,0:T(8,128)S(1)} %get-tuple-element.120), channel_id=1, source_target_pairs={{0,8},{8,16},{16,24},{1,9},{9,17},{17,25},{2,10},{10,18},{18,26},{... | collective-permute-start | bytes 12296 | tf_op jit(solution)/shard_map/ppermute | solution.py:18
  193.7 4.3 %collective-permute-start.14 = (f32[6,1,128]{2,1,0:T(1,128)S(1)}, f32[6,1,128]{2,1,0:T(1,128)S(1)}, u32[]{:S(2)}, u32[]{:S(2)}) collective-permute-start(f32[6,1,128]{2,1,0:T(1,128)S(1)} %get-tuple-element.115), channel_id=1, source_target_pairs={{2,0},{4,2},{6,4},{3,1},{5,3},{7,5},{10,8},{12,10},{14,12},{11,9},... | collective-permute-start | bytes 9224 | tf_op jit(solution)/shard_map/ppermute | solution.py:19
  195.0 3.8 %collective-permute-start.15 = (f32[6,1,128]{2,1,0:T(1,128)S(1)}, f32[6,1,128]{2,1,0:T(1,128)S(1)}, u32[]{:S(2)}, u32[]{:S(2)}) collective-permute-start(f32[6,1,128]{2,1,0:T(1,128)S(1)} %get-tuple-element.114), channel_id=1, source_target_pairs={{0,2},{2,4},{4,6},{1,3},{3,5},{5,7},{8,10},{10,12},{12,14},{9,11},... | collective-permute-start | bytes 9224 | tf_op jit(solution)/shard_map/ppermute | solution.py:18
  198.9 6.1 %collective-permute-start.17 = (f32[6,10,1]{2,1,0:T(8,128)S(1)}, f32[6,10,1]{2,1,0:T(8,128)S(1)}, u32[]{:S(2)}, u32[]{:S(2)}) collective-permute-start(f32[6,10,1]{2,1,0:T(8,128)S(1)} %get-tuple-element.109), channel_id=1, source_target_pairs={{0,1},{2,3},{4,5},{6,7},{8,9},{10,11},{12,13},{14,15},{16,17},{18,... | collective-permute-start | bytes 728 | tf_op jit(solution)/shard_map/ppermute | solution.py:18
  203.3 6.3 %collective-permute-start.16 = (f32[6,10,1]{2,1,0:T(8,128)S(1)}, f32[6,10,1]{2,1,0:T(8,128)S(1)}, u32[]{:S(2)}, u32[]{:S(2)}) collective-permute-start(f32[6,10,1]{2,1,0:T(8,128)S(1)} %get-tuple-element.108), channel_id=1, source_target_pairs={{1,0},{3,2},{5,4},{7,6},{9,8},{11,10},{13,12},{15,14},{17,16},{19,... | collective-permute-start | bytes 728 | tf_op jit(solution)/shard_map/ppermute | solution.py:19
where the time goes:
time: 260 us; the launch traced here: 258 us
  blocking collectives  166 us (64%)
  starting transfers between devices  47.2 us (18%)
  waiting for transfers between devices  19.5 us (8%)
  matrix products  10.7 us (4%)
  between operations  7.79 us (3%)
  local copies, waits for them, and re-layouts  4 us (2%)
  other arithmetic  3.24 us (1%)
    psum x3, blocking collectives, per_device(): lax.psum((jnp.dot(flat_basis, applied, precision=highest), jnp.sum(applie...  124 us
    psum x1, blocking collectives, per_device(): lax.psum(jnp.dot(flat_start, flat_start.T, precision=highest), ('gx', 'gy...  42.1 us
    ppermute x9, starting transfers between devices, with_halo(): before = lax.ppermute(last, axis, up)  35.6 us
    ppermute x9, waiting for transfers between devices, with_halo(): after = lax.ppermute(initial, axis, down)  13.4 us
    ppermute x9, starting transfers between devices, with_halo(): after = lax.ppermute(initial, axis, down)  11.6 us
    ppermute x9, waiting for transfers between devices, with_halo(): before = lax.ppermute(last, axis, up)  6.12 us
  transfers between devices with their start and end apart: 18, of which 12 were waited for; matrix products, arithmetic and copies ran while one was open for 0% of the time, Pallas kernels for 0%

commit v1 on v0

--- a/solution.py
+++ b/solution.py
@@ -6,6 +6,12 @@
 KEEP = 20
 EXPAND = 3
 ROWS = 24
+
+
+def views_order(local_x):
+    for j0 in (("gy", "gz"), "gx"):
+        local_x = lax.psum(local_x, j0)
+    return local_x
 
 
 def with_halo(value, sides, width):
@@ -75,9 +81,8 @@
         count = vectors.shape[0]
         flat_basis = vectors.reshape(count, -1)
         applied = operate_field(vectors[-1], diag_shift, velocity).reshape(-1)
-        dotted, self_sum = lax.psum(
-            (jnp.dot(flat_basis, applied, precision=highest), jnp.sum(applied * applied)),
-            ("gx", "gy", "gz"),
+        dotted, self_sum = views_order(
+            (jnp.dot(flat_basis, applied, precision=highest), jnp.sum(applied * applied))
         )
         first_coeffs = dotted / cell_count
         self_norm = self_sum / cell_count

time: 260 us -> 211 us (0.81)
  blocking collectives: 166 us -> 119 us
    psum x3 -> x6, blocking collectives: 124 us -> 76.5 us  [views_order(): local_x = lax.psum(local_x, j0)]
  transfers between devices with their start and end apart: 18 -> 18, of which waited for: 12 -> 12; matrix products, arithmetic and copies ran while one was open for 0% -> 1% of each run, Pallas kernels for 0% -> 0%
where the time goes in v1:
time: 211 us; the launch traced here: 210 us
  blocking collectives  119 us (56%)
  starting transfers between devices  46.8 us (22%)
  waiting for transfers between devices  19.1 us (9%)
  matrix products  10.7 us (5%)
  between operations  7.84 us (4%)
  local copies, waits for them, and re-layouts  4 us (2%)
  other arithmetic  3.24 us (2%)
    psum x6, blocking collectives, views_order(): local_x = lax.psum(local_x, j0)  76.5 us
    psum x1, blocking collectives, per_device(): lax.psum(jnp.dot(flat_start, flat_start.T, precision=highest), ('gx', 'gy...  42.1 us
    ppermute x9, starting transfers between devices, with_halo(): before = lax.ppermute(last, axis, up)  35.2 us
    ppermute x9, waiting for transfers between devices, with_halo(): after = lax.ppermute(initial, axis, down)  13 us
    ppermute x9, starting transfers between devices, with_halo(): after = lax.ppermute(initial, axis, down)  11.6 us
    ppermute x9, waiting for transfers between devices, with_halo(): before = lax.ppermute(last, axis, up)  6.12 us
  transfers between devices with their start and end apart: 18, of which 12 were waited for; matrix products, arithmetic and copies ran while one was open for 1% of the time, Pallas kernels for 0%

profile of v1, /device:TPU:0, one launch (start us, length us, event | category | flops | bytes accessed | tf_op | source)
XLA Modules:
  0.0 210.3 jit_solution(16777343644042464563)
XLA Ops:
  0.7 1.2 copy-done
  1.8 1.9 fusion.10
  3.7 0.5 convolution_bitcast_fusion
  4.2 42.1 %psum.91 = f32[21,21]{1,0:T(8,128)S(1)} all-reduce(f32[21,21]{1,0:T(8,128)S(1)} %convolution_bitcast_fusion), channel_id=1, replica_groups=mesh['gx'=4,'gy'=4,'gz'=2] {'gx','gy','gz'}, use_global_device_ids=true, to_apply=%region_0.0 | all-reduce | flops 441 | bytes 3528 | tf_op jit(solution)/shard_map/psum | solution.py:73
  46.3 0.6 slice.304
  47.6 1.3 collective-permute-start
  48.9 4.5 %collective-permute-start.1 = (f32[1,8,128]{2,1,0:T(8,128)S(1)}, f32[1,8,128]{2,1,0:T(8,128)S(1)}, u32[]{:S(2)}, u32[]{:S(2)}) collective-permute-start(f32[1,8,128]{2,1,0:T(8,128)S(1)} %get-tuple-element.130), channel_id=1, source_target_pairs={{0,8},{8,16},{16,24},{1,9},{9,17},{17,25},{2,10},{10,18},{18,26},{... | collective-permute-start | bytes 12296 | tf_op jit(solution)/shard_map/ppermute | solution.py:24
  53.7 1.1 collective-permute-done.1
  54.8 1.3 collective-permute-start.2
  56.1 3.0 %collective-permute-start.3 = (f32[6,1,128]{2,1,0:T(1,128)S(1)}, f32[6,1,128]{2,1,0:T(1,128)S(1)}, u32[]{:S(2)}, u32[]{:S(2)}) collective-permute-start(f32[6,1,128]{2,1,0:T(1,128)S(1)} %get-tuple-element.124), channel_id=1, source_target_pairs={{0,2},{2,4},{4,6},{1,3},{3,5},{5,7},{8,10},{10,12},{12,14},{9,11},... | collective-permute-start | bytes 9224 | tf_op jit(solution)/shard_map/ppermute | solution.py:24
  59.3 0.7 collective-permute-done.3
  60.0 4.2 %collective-permute-start.5 = (f32[6,10,1]{2,1,0:T(8,128)S(1)}, f32[6,10,1]{2,1,0:T(8,128)S(1)}, u32[]{:S(2)}, u32[]{:S(2)}) collective-permute-start(f32[6,10,1]{2,1,0:T(8,128)S(1)} %get-tuple-element.119), channel_id=1, source_target_pairs={{0,1},{2,3},{4,5},{6,7},{8,9},{10,11},{12,13},{14,15},{16,17},{18,... | collective-permute-start | bytes 728 | tf_op jit(solution)/shard_map/ppermute | solution.py:24
  64.2 1.3 collective-permute-start.4
  65.6 0.2 copy.36
  66.0 4.3 %collective-permute-done.4 = f32[6,10,1]{2,1,0:T(8,128)S(1)} collective-permute-done((f32[6,10,1]{2,1,0:T(8,128)S(1)}, f32[6,10,1]{2,1,0:T(8,128)S(1)}, u32[]{:S(2)}, u32[]{:S(2)}) %collective-permute-start.4) | collective-permute-done | bytes 272 | tf_op jit(solution)/shard_map/ppermute | solution.py:25
  70.2 0.7 multiply_reduce_fusion.2
  70.9 0.5 convolution_bitcast_fusion.11
  71.4 12.6 %all-reduce.6 = (f32[21]{0:T(128)S(1)}, f32[]{:T(128)}) all-reduce(f32[21]{0:T(128)S(1)} %convolution_bitcast_fusion.11, f32[]{:T(128)} %get-tuple-element.112), channel_id=1, replica_groups=mesh['gx'=4,'gy'=4,'gz'=2] {'gy','gz'}, use_global_device_ids=true, to_apply=%region_1.0 | all-reduce | flops 22 | bytes 176 | tf_op jit(solution)/shard_map/psum | solution.py:13
  84.0 13.0 %all-reduce.9 = (f32[21]{0:T(128)S(1)}, f32[]{:T(128)}) all-reduce(f32[21]{0:T(128)S(1)} %get-tuple-element.94, f32[]{:T(128)} %get-tuple-element.95), channel_id=1, replica_groups=mesh['gx'=4,'gy'=4,'gz'=2] {'gx'}, use_global_device_ids=true, to_apply=%region_2.0 | all-reduce | flops 22 | bytes 176 | tf_op jit(solution)/shard_map/psum | solution.py:13
  97.0 0.7 multiply_reduce_fusion.5
  97.8 0.3 fusion.34
  98.1 0.3 fusion.33
  99.1 0.7 fusion.12
  101.2 0.1 fusion.8
  101.3 1.3 collective-permute-start.6
  102.6 4.5 %collective-permute-start.7 = (f32[1,8,128]{2,1,0:T(8,128)S(1)}, f32[1,8,128]{2,1,0:T(8,128)S(1)}, u32[]{:S(2)}, u32[]{:S(2)}) collective-permute-start(f32[1,8,128]{2,1,0:T(8,128)S(1)} %get-tuple-element.128), channel_id=1, source_target_pairs={{0,8},{8,16},{16,24},{1,9},{9,17},{17,25},{2,10},{10,18},{18,26},{... | collective-permute-start | bytes 12296 | tf_op jit(solution)/shard_map/ppermute | solution.py:24
  107.5 1.0 collective-permute-done.7
  108.5 1.3 collective-permute-start.8
  109.8 3.0 %collective-permute-start.9 = (f32[6,1,128]{2,1,0:T(1,128)S(1)}, f32[6,1,128]{2,1,0:T(1,128)S(1)}, u32[]{:S(2)}, u32[]{:S(2)}) collective-permute-start(f32[6,1,128]{2,1,0:T(1,128)S(1)} %get-tuple-element.122), channel_id=1, source_target_pairs={{0,2},{2,4},{4,6},{1,3},{3,5},{5,7},{8,10},{10,12},{12,14},{9,11},... | collective-permute-start | bytes 9224 | tf_op jit(solution)/shard_map/ppermute | solution.py:24
  112.9 0.8 collective-permute-done.9
  113.7 4.1 %collective-permute-start.11 = (f32[6,10,1]{2,1,0:T(8,128)S(1)}, f32[6,10,1]{2,1,0:T(8,128)S(1)}, u32[]{:S(2)}, u32[]{:S(2)}) collective-permute-start(f32[6,10,1]{2,1,0:T(8,128)S(1)} %get-tuple-element.117), channel_id=1, source_target_pairs={{0,1},{2,3},{4,5},{6,7},{8,9},{10,11},{12,13},{14,15},{16,17},{18,... | collective-permute-start | bytes 728 | tf_op jit(solution)/shard_map/ppermute | solution.py:24
  117.8 1.3 collective-permute-start.10
  119.3 0.3 collective-permute-done.11
  119.6 4.3 %collective-permute-done.10 = f32[6,10,1]{2,1,0:T(8,128)S(1)} collective-permute-done((f32[6,10,1]{2,1,0:T(8,128)S(1)}, f32[6,10,1]{2,1,0:T(8,128)S(1)}, u32[]{:S(2)}, u32[]{:S(2)}) %collective-permute-start.10) | collective-permute-done | bytes 272 | tf_op jit(solution)/shard_map/ppermute | solution.py:25
  123.8 0.7 multiply_reduce_fusion.1
  124.5 0.5 convolution_bitcast_fusion.10
  125.0 14.4 %all-reduce.5 = (f32[22]{0:T(128)S(1)}, f32[]{:T(128)}) all-reduce(f32[22]{0:T(128)S(1)} %convolution_bitcast_fusion.10, f32[]{:T(128)} %get-tuple-element.108), channel_id=1, replica_groups=mesh['gx'=4,'gy'=4,'gz'=2] {'gy','gz'}, use_global_device_ids=true, to_apply=%region_6.0 | all-reduce | flops 23 | bytes 184 | tf_op jit(solution)/shard_map/psum | solution.py:13
  139.4 11.2 %all-reduce.8 = (f32[22]{0:T(128)S(1)}, f32[]{:T(128)}) all-reduce(f32[22]{0:T(128)S(1)} %get-tuple-element.92, f32[]{:T(128)} %get-tuple-element.93), channel_id=1, replica_groups=mesh['gx'=4,'gy'=4,'gz'=2] {'gx'}, use_global_device_ids=true, to_apply=%region_7.0 | all-reduce | flops 23 | bytes 184 | tf_op jit(solution)/shard_map/psum | solution.py:13
  150.7 0.7 multiply_reduce_fusion.4
  151.4 0.4 fusion.36
  151.8 0.4 fusion.35
  153.4 0.7 fusion.13
  154.8 0.1 fusion.9
  155.0 1.3 collective-permute-start.12
  156.3 4.5 %collective-permute-start.13 = (f32[1,8,128]{2,1,0:T(8,128)S(1)}, f32[1,8,128]{2,1,0:T(8,128)S(1)}, u32[]{:S(2)}, u32[]{:S(2)}) collective-permute-start(f32[1,8,128]{2,1,0:T(8,128)S(1)} %get-tuple-element.126), channel_id=1, source_target_pairs={{0,8},{8,16},{16,24},{1,9},{9,17},{17,25},{2,10},{10,18},{18,26},{... | collective-permute-start | bytes 12296 | tf_op jit(solution)/shard_map/ppermute | solution.py:24
  161.2 1.0 collective-permute-done.13
  162.2 1.3 collective-permute-start.14
  163.5 3.0 %collective-permute-start.15 = (f32[6,1,128]{2,1,0:T(1,128)S(1)}, f32[6,1,128]{2,1,0:T(1,128)S(1)}, u32[]{:S(2)}, u32[]{:S(2)}) collective-permute-start(f32[6,1,128]{2,1,0:T(1,128)S(1)} %get-tuple-element.120), channel_id=1, source_target_pairs={{0,2},{2,4},{4,6},{1,3},{3,5},{5,7},{8,10},{10,12},{12,14},{9,11},... | collective-permute-start | bytes 9224 | tf_op jit(solution)/shard_map/ppermute | solution.py:24
  166.5 0.8 collective-permute-done.15
  167.4 4.2 %collective-permute-start.17 = (f32[6,10,1]{2,1,0:T(8,128)S(1)}, f32[6,10,1]{2,1,0:T(8,128)S(1)}, u32[]{:S(2)}, u32[]{:S(2)}) collective-permute-start(f32[6,10,1]{2,1,0:T(8,128)S(1)} %get-tuple-element.115), channel_id=1, source_target_pairs={{0,1},{2,3},{4,5},{6,7},{8,9},{10,11},{12,13},{14,15},{16,17},{18,... | collective-permute-start | bytes 728 | tf_op jit(solution)/shard_map/ppermute | solution.py:24
  171.6 1.3 collective-permute-start.16
  173.0 0.3 collective-permute-done.17
  173.3 4.4 %collective-permute-done.16 = f32[6,10,1]{2,1,0:T(8,128)S(1)} collective-permute-done((f32[6,10,1]{2,1,0:T(8,128)S(1)}, f32[6,10,1]{2,1,0:T(8,128)S(1)}, u32[]{:S(2)}, u32[]{:S(2)}) %collective-permute-start.16) | collective-permute-done | bytes 272 | tf_op jit(solution)/shard_map/ppermute | solution.py:25
  177.8 0.7 multiply_reduce_fusion
  178.5 0.5 convolution_bitcast_fusion.9
  179.0 14.0 %all-reduce.4 = (f32[23]{0:T(128)S(1)}, f32[]{:T(128)}) all-reduce(f32[23]{0:T(128)S(1)} %convolution_bitcast_fusion.9, f32[]{:T(128)} %get-tuple-element.104), channel_id=1, replica_groups=mesh['gx'=4,'gy'=4,'gz'=2] {'gy','gz'}, use_global_device_ids=true, to_apply=%region_11.0 | all-reduce | flops 24 | bytes 192 | tf_op jit(solution)/shard_map/psum | solution.py:13
  193.0 11.2 %all-reduce.7 = (f32[23]{0:T(128)S(1)}, f32[]{:T(128)}) all-reduce(f32[23]{0:T(128)S(1)} %get-tuple-element.90, f32[]{:T(128)} %get-tuple-element.91), channel_id=1, replica_groups=mesh['gx'=4,'gy'=4,'gz'=2] {'gx'}, use_global_device_ids=true, to_apply=%region_12.0 | all-reduce | flops 24 | bytes 192 | tf_op jit(solution)/shard_map/psum | solution.py:13
  204.2 0.7 multiply_reduce_fusion.3
  205.0 0.8 fusion.14
  205.8 0.4 fusion.38
  206.2 0.4 fusion.37
  208.6 0.2 concatenate.183
  208.8 0.8 copy.15
  209.7 0.6 pad_maximum_fusion.77
  (47 shorter events, 1.7 us)
Async XLA Ops:
  0.6 1.2 copy-start
  0.6 3.1 %copy-start.3 = (f32[4,8,128]{2,1,0:T(8,128)S(1)}, f32[4,8,128]{2,1,0:T(8,128)}, u32[]{:S(2)}) copy-start(f32[4,8,128]{2,1,0:T(8,128)} %param.21) | copy-start | bytes 49156
  47.6 6.1 %collective-permute-start = (f32[1,8,128]{2,1,0:T(8,128)S(1)}, f32[1,8,128]{2,1,0:T(8,128)S(1)}, u32[]{:S(2)}, u32[]{:S(2)}) collective-permute-start(f32[1,8,128]{2,1,0:T(8,128)S(1)} %get-tuple-element.131), channel_id=1, source_target_pairs={{8,0},{16,8},{24,16},{9,1},{17,9},{25,17},{10,2},{18,10},{26,18},{... | collective-permute-start | bytes 12296 | tf_op jit(solution)/shard_map/ppermute | solution.py:25
  48.9 5.9 %collective-permute-start.1 = (f32[1,8,128]{2,1,0:T(8,128)S(1)}, f32[1,8,128]{2,1,0:T(8,128)S(1)}, u32[]{:S(2)}, u32[]{:S(2)}) collective-permute-start(f32[1,8,128]{2,1,0:T(8,128)S(1)} %get-tuple-element.130), channel_id=1, source_target_pairs={{0,8},{8,16},{16,24},{1,9},{9,17},{17,25},{2,10},{10,18},{18,26},{... | collective-permute-start | bytes 12296 | tf_op jit(solution)/shard_map/ppermute | solution.py:24
  54.8 4.5 %collective-permute-start.2 = (f32[6,1,128]{2,1,0:T(1,128)S(1)}, f32[6,1,128]{2,1,0:T(1,128)S(1)}, u32[]{:S(2)}, u32[]{:S(2)}) collective-permute-start(f32[6,1,128]{2,1,0:T(1,128)S(1)} %get-tuple-element.125), channel_id=1, source_target_pairs={{2,0},{4,2},{6,4},{3,1},{5,3},{7,5},{10,8},{12,10},{14,12},{11,9},... | collective-permute-start | bytes 9224 | tf_op jit(solution)/shard_map/ppermute | solution.py:25
  56.1 3.8 %collective-permute-start.3 = (f32[6,1,128]{2,1,0:T(1,128)S(1)}, f32[6,1,128]{2,1,0:T(1,128)S(1)}, u32[]{:S(2)}, u32[]{:S(2)}) collective-permute-start(f32[6,1,128]{2,1,0:T(1,128)S(1)} %get-tuple-element.124), channel_id=1, source_target_pairs={{0,2},{2,4},{4,6},{1,3},{3,5},{5,7},{8,10},{10,12},{12,14},{9,11},... | collective-permute-start | bytes 9224 | tf_op jit(solution)/shard_map/ppermute | solution.py:24
  60.0 5.9 %collective-permute-start.5 = (f32[6,10,1]{2,1,0:T(8,128)S(1)}, f32[6,10,1]{2,1,0:T(8,128)S(1)}, u32[]{:S(2)}, u32[]{:S(2)}) collective-permute-start(f32[6,10,1]{2,1,0:T(8,128)S(1)} %get-tuple-element.119), channel_id=1, source_target_pairs={{0,1},{2,3},{4,5},{6,7},{8,9},{10,11},{12,13},{14,15},{16,17},{18,... | collective-permute-start | bytes 728 | tf_op jit(solution)/shard_map/ppermute | solution.py:24
  64.2 6.0 %collective-permute-start.4 = (f32[6,10,1]{2,1,0:T(8,128)S(1)}, f32[6,10,1]{2,1,0:T(8,128)S(1)}, u32[]{:S(2)}, u32[]{:S(2)}) collective-permute-start(f32[6,10,1]{2,1,0:T(8,128)S(1)} %get-tuple-element.118), channel_id=1, source_target_pairs={{1,0},{3,2},{5,4},{7,6},{9,8},{11,10},{13,12},{15,14},{17,16},{19,... | collective-permute-start | bytes 728 | tf_op jit(solution)/shard_map/ppermute | solution.py:25
  65.6 4.6 %copy-start.1 = (f32[3,4,8,128]{3,2,1,0:T(8,128)S(1)}, f32[3,4,8,128]{3,2,1,0:T(8,128)}, u32[]{:S(2)}) copy-start(f32[3,4,8,128]{3,2,1,0:T(8,128)} %param.23) | copy-start | bytes 147460
  65.6 4.6 %copy-start.2 = (f32[4,8,128]{2,1,0:T(8,128)S(1)}, f32[4,8,128]{2,1,0:T(8,128)}, u32[]{:S(2)}) copy-start(f32[4,8,128]{2,1,0:T(8,128)} %param.22) | copy-start | bytes 49156
  101.3 6.2 %collective-permute-start.6 = (f32[1,8,128]{2,1,0:T(8,128)S(1)}, f32[1,8,128]{2,1,0:T(8,128)S(1)}, u32[]{:S(2)}, u32[]{:S(2)}) collective-permute-start(f32[1,8,128]{2,1,0:T(8,128)S(1)} %get-tuple-element.129), channel_id=1, source_target_pairs={{8,0},{16,8},{24,16},{9,1},{17,9},{25,17},{10,2},{18,10},{26,18},{... | collective-permute-start | bytes 12296 | tf_op jit(solution)/shard_map/ppermute | solution.py:25
  102.6 5.9 %collective-permute-start.7 = (f32[1,8,128]{2,1,0:T(8,128)S(1)}, f32[1,8,128]{2,1,0:T(8,128)S(1)}, u32[]{:S(2)}, u32[]{:S(2)}) collective-permute-start(f32[1,8,128]{2,1,0:T(8,128)S(1)} %get-tuple-element.128), channel_id=1, source_target_pairs={{0,8},{8,16},{16,24},{1,9},{9,17},{17,25},{2,10},{10,18},{18,26},{... | collective-permute-start | bytes 12296 | tf_op jit(solution)/shard_map/ppermute | solution.py:24
  108.5 4.3 %collective-permute-start.8 = (f32[6,1,128]{2,1,0:T(1,128)S(1)}, f32[6,1,128]{2,1,0:T(1,128)S(1)}, u32[]{:S(2)}, u32[]{:S(2)}) collective-permute-start(f32[6,1,128]{2,1,0:T(1,128)S(1)} %get-tuple-element.123), channel_id=1, source_target_pairs={{2,0},{4,2},{6,4},{3,1},{5,3},{7,5},{10,8},{12,10},{14,12},{11,9},... | collective-permute-start | bytes 9224 | tf_op jit(solution)/shard_map/ppermute | solution.py:25
  109.8 3.8 %collective-permute-start.9 = (f32[6,1,128]{2,1,0:T(1,128)S(1)}, f32[6,1,128]{2,1,0:T(1,128)S(1)}, u32[]{:S(2)}, u32[]{:S(2)}) collective-permute-start(f32[6,1,128]{2,1,0:T(1,128)S(1)} %get-tuple-element.122), channel_id=1, source_target_pairs={{0,2},{2,4},{4,6},{1,3},{3,5},{5,7},{8,10},{10,12},{12,14},{9,11},... | collective-permute-start | bytes 9224 | tf_op jit(solution)/shard_map/ppermute | solution.py:24
  113.7 5.8 %collective-permute-start.11 = (f32[6,10,1]{2,1,0:T(8,128)S(1)}, f32[6,10,1]{2,1,0:T(8,128)S(1)}, u32[]{:S(2)}, u32[]{:S(2)}) collective-permute-start(f32[6,10,1]{2,1,0:T(8,128)S(1)} %get-tuple-element.117), channel_id=1, source_target_pairs={{0,1},{2,3},{4,5},{6,7},{8,9},{10,11},{12,13},{14,15},{16,17},{18,... | collective-permute-start | bytes 728 | tf_op jit(solution)/shard_map/ppermute | solution.py:24
  117.8 6.0 %collective-permute-start.10 = (f32[6,10,1]{2,1,0:T(8,128)S(1)}, f32[6,10,1]{2,1,0:T(8,128)S(1)}, u32[]{:S(2)}, u32[]{:S(2)}) collective-permute-start(f32[6,10,1]{2,1,0:T(8,128)S(1)} %get-tuple-element.116), channel_id=1, source_target_pairs={{1,0},{3,2},{5,4},{7,6},{9,8},{11,10},{13,12},{15,14},{17,16},{19,... | collective-permute-start | bytes 728 | tf_op jit(solution)/shard_map/ppermute | solution.py:25
  155.0 6.2 %collective-permute-start.12 = (f32[1,8,128]{2,1,0:T(8,128)S(1)}, f32[1,8,128]{2,1,0:T(8,128)S(1)}, u32[]{:S(2)}, u32[]{:S(2)}) collective-permute-start(f32[1,8,128]{2,1,0:T(8,128)S(1)} %get-tuple-element.127), channel_id=1, source_target_pairs={{8,0},{16,8},{24,16},{9,1},{17,9},{25,17},{10,2},{18,10},{26,18},{... | collective-permute-start | bytes 12296 | tf_op jit(solution)/shard_map/ppermute | solution.py:25
  156.3 5.9 %collective-permute-start.13 = (f32[1,8,128]{2,1,0:T(8,128)S(1)}, f32[1,8,128]{2,1,0:T(8,128)S(1)}, u32[]{:S(2)}, u32[]{:S(2)}) collective-permute-start(f32[1,8,128]{2,1,0:T(8,128)S(1)} %get-tuple-element.126), channel_id=1, source_target_pairs={{0,8},{8,16},{16,24},{1,9},{9,17},{17,25},{2,10},{10,18},{18,26},{... | collective-permute-start | bytes 12296 | tf_op jit(solution)/shard_map/ppermute | solution.py:24
  162.2 4.3 %collective-permute-start.14 = (f32[6,1,128]{2,1,0:T(1,128)S(1)}, f32[6,1,128]{2,1,0:T(1,128)S(1)}, u32[]{:S(2)}, u32[]{:S(2)}) collective-permute-start(f32[6,1,128]{2,1,0:T(1,128)S(1)} %get-tuple-element.121), channel_id=1, source_target_pairs={{2,0},{4,2},{6,4},{3,1},{5,3},{7,5},{10,8},{12,10},{14,12},{11,9},... | collective-permute-start | bytes 9224 | tf_op jit(solution)/shard_map/ppermute | solution.py:25
  163.5 3.8 %collective-permute-start.15 = (f32[6,1,128]{2,1,0:T(1,128)S(1)}, f32[6,1,128]{2,1,0:T(1,128)S(1)}, u32[]{:S(2)}, u32[]{:S(2)}) collective-permute-start(f32[6,1,128]{2,1,0:T(1,128)S(1)} %get-tuple-element.120), channel_id=1, source_target_pairs={{0,2},{2,4},{4,6},{1,3},{3,5},{5,7},{8,10},{10,12},{12,14},{9,11},... | collective-permute-start | bytes 9224 | tf_op jit(solution)/shard_map/ppermute | solution.py:24
  167.4 5.9 %collective-permute-start.17 = (f32[6,10,1]{2,1,0:T(8,128)S(1)}, f32[6,10,1]{2,1,0:T(8,128)S(1)}, u32[]{:S(2)}, u32[]{:S(2)}) collective-permute-start(f32[6,10,1]{2,1,0:T(8,128)S(1)} %get-tuple-element.115), channel_id=1, source_target_pairs={{0,1},{2,3},{4,5},{6,7},{8,9},{10,11},{12,13},{14,15},{16,17},{18,... | collective-permute-start | bytes 728 | tf_op jit(solution)/shard_map/ppermute | solution.py:24
  171.6 6.2 %collective-permute-start.16 = (f32[6,10,1]{2,1,0:T(8,128)S(1)}, f32[6,10,1]{2,1,0:T(8,128)S(1)}, u32[]{:S(2)}, u32[]{:S(2)}) collective-permute-start(f32[6,10,1]{2,1,0:T(8,128)S(1)} %get-tuple-element.114), channel_id=1, source_target_pairs={{1,0},{3,2},{5,4},{7,6},{9,8},{11,10},{13,12},{15,14},{17,16},{19,... | collective-permute-start | bytes 728 | tf_op jit(solution)/shard_map/ppermute | solution.py:25
